TPU v7x, 128 devices: a whole 4x4x4 slice. The times are simulated.
128 devices in a mesh: section: 4 (over y_hi, core), fsdp: 32 (over z, x, y_lo).
Axes of the slice: x: 4, y: 4 (y_hi: 2, y_lo: 2; y = y_hi * 2 + y_lo), z: 4, core: 2. Of those that a mesh axis runs over, the one named last changes fastest.
Arguments:
- hidden_in: bfloat16 [4096, 4096], P('fsdp'), may hold values from -6 to 6
- out_grad: bfloat16 [4096, 4096], P('fsdp'), may hold values from -6 to 6
- fast_in: float32 [4, 4096, 1024], P('section', 'fsdp'), may hold values from -6 to 6
- fast_out: float32 [4, 1024, 4096], P('section', None, 'fsdp'), may hold values from -6 to 6
- slow_in: float32 [4, 4096, 1024], P('section', 'fsdp'), may hold values from -6 to 6
- slow_out: float32 [4, 1024, 4096], P('section', None, 'fsdp'), may hold values from -6 to 6
Outputs:
- section_out: bfloat16 [4, 4096, 4096], P('section', 'fsdp')
- input_grad: bfloat16 [4, 4096, 4096], P('section', 'fsdp')
- synced_in: float32 [4, 4096, 1024], P('section', 'fsdp')
- synced_out: float32 [4, 1024, 4096], P('section', None, 'fsdp')
All inputs are finite; a program needn't handle non-finite values.
Results may differ from a plain program's by a relative error of at most 0.014.
Values may be sent and summed in bfloat16 or wider, within the bound.
A program may use at most 896 MiB of HBM per device.

v0:
```python
import math
import jax
import jax.numpy as jnp
from jax import lax
from jax.sharding import PartitionSpec as P

epsilon = 1e-05
fast_rate = 0.5
preview_mix = 0.5


def gather_turned(arrays, axis, dims):
    turned = [jnp.moveaxis(a, dim, 0) for a, dim in zip(arrays, dims)]
    widths = [t[0].size for t in turned]
    both = jnp.concatenate([t.reshape(-1, w) for t, w in zip(turned, widths)], axis=1)
    result = lax.all_gather(both, axis, axis=0, tiled=True)
    pieces = jnp.split(result, [sum(widths[:k]) for k in range(1, len(widths))], axis=1)
    return tuple(
        (
            jnp.moveaxis(b.reshape(-1, *t.shape[1:]), 0, dim)
            for b, t, dim in zip(pieces, turned, dims)
        )
    )


def from_behind(value, axis, steps):
    count = lax.axis_size(axis)
    leading, last = (max(0, -steps), min(count, count - steps))
    return lax.ppermute(value, axis, [(source, source + steps) for source in range(leading, last)])


def contract_last(left_rows, right_rows):
    return lax.dot_general(
        left_rows, right_rows, (((1,), (1,)), ((), ())), preferred_element_type=jnp.float32
    )


def contract_first(left_rows, right_rows):
    return lax.dot_general(
        left_rows, right_rows, (((0,), (0,)), ((), ())), preferred_element_type=jnp.float32
    )


def prepare(hidden, weight_in):
    widened = hidden.astype(jnp.float32)
    inverse_rms = lax.rsqrt(jnp.mean(widened * widened, axis=-1, keepdims=True) + epsilon)
    normed = (widened * inverse_rms).astype(jnp.bfloat16)
    pre_act = jnp.dot(normed, weight_in, preferred_element_type=jnp.float32)
    activated = jax.nn.silu(pre_act).astype(jnp.bfloat16)
    return (widened, inverse_rms, normed, pre_act, activated)


def advance(hidden, weight_in, weight_out):
    widened, inverse_rms, normed, pre_act, activated = prepare(hidden, weight_in)
    return (widened + jnp.dot(activated, weight_out, preferred_element_type=jnp.float32)).astype(
        jnp.bfloat16
    )


def retreat(hidden, cot_in, weight_in, weight_out):
    widened, inverse_rms, normed, pre_act, activated = prepare(hidden, weight_in)
    act_grad = contract_last(cot_in, weight_out)
    sigmoid_vals = jax.nn.sigmoid(pre_act)
    pre_grad = (act_grad * sigmoid_vals * (1.0 + pre_act * (1.0 - sigmoid_vals))).astype(
        jnp.bfloat16
    )
    norm_grad = contract_last(pre_grad, weight_in)
    unit_rows = widened * inverse_rms
    rms_grad = inverse_rms * (
        norm_grad - unit_rows * jnp.mean(norm_grad * unit_rows, axis=-1, keepdims=True)
    )
    earlier = (cot_in.astype(jnp.float32) + rms_grad).astype(jnp.bfloat16)
    return (earlier, contract_first(normed, pre_grad), contract_first(activated, cot_in))


def shards(hidden_in, out_grad, fast_in, fast_out, slow_in, slow_out):
    sections = lax.axis_size("section")
    section_index = lax.axis_index("section")
    row_count, model_width = hidden_in.shape
    branch_units = fast_in.shape[2]
    in_scale = 1.0 / math.sqrt(model_width)
    out_scale = 1.0 / math.sqrt(branch_units)
    local_in = (fast_in[0] * in_scale).astype(jnp.bfloat16)
    local_out = (fast_out[0] * out_scale).astype(jnp.bfloat16)
    weight_in, weight_out = gather_turned((local_in, local_out), "fsdp", (0, 1))
    portions = 1
    block_rows = row_count // portions
    turn_count = sections + portions - 1
    sources = hidden_in.reshape(portions, block_rows, model_width)
    targets = out_grad.reshape(portions, block_rows, model_width)
    saved_inputs = jnp.zeros_like(sources)
    produced = jnp.zeros_like(sources)
    incoming = jnp.zeros((block_rows, model_width), jnp.bfloat16)
    for timestep in range(turn_count):
        block_slot = timestep - section_index
        active = (block_slot >= 0) & (block_slot < portions)
        block_index = jnp.clip(block_slot, 0, portions - 1)
        first_input = lax.dynamic_index_in_dim(sources, block_index, 0, keepdims=False)
        section_input = jnp.where(section_index == 0, first_input, incoming)

        def run_forward():
            return advance(section_input, weight_in, weight_out)

        def skip_forward():
            return jnp.zeros_like(section_input)

        section_output = lax.cond(active, run_forward, skip_forward)
        saved_inputs = jnp.where(
            active,
            lax.dynamic_update_index_in_dim(saved_inputs, section_input, block_index, 0),
            saved_inputs,
        )
        produced = jnp.where(
            active,
            lax.dynamic_update_index_in_dim(produced, section_output, block_index, 0),
            produced,
        )
        if timestep + 1 < turn_count:
            incoming = from_behind(section_output, "section", 1)
    grad_in = jnp.zeros((model_width, branch_units), jnp.float32)
    grad_out = jnp.zeros((branch_units, model_width), jnp.float32)
    cotangents = jnp.zeros_like(sources)
    incoming = jnp.zeros((block_rows, model_width), jnp.bfloat16)
    for timestep in range(turn_count):
        block_slot = timestep - (sections - 1 - section_index)
        active = (block_slot >= 0) & (block_slot < portions)
        block_index = jnp.clip(block_slot, 0, portions - 1)
        last_cot = lax.dynamic_index_in_dim(targets, block_index, 0, keepdims=False)
        cot_in = jnp.where(section_index == sections - 1, last_cot, incoming)
        hidden = lax.dynamic_index_in_dim(saved_inputs, block_index, 0, keepdims=False)

        def run_backward():
            return retreat(hidden, cot_in, weight_in, weight_out)

        def skip_backward():
            return (
                jnp.zeros_like(cot_in),
                jnp.zeros((model_width, branch_units), jnp.float32),
                jnp.zeros((branch_units, model_width), jnp.float32),
            )

        earlier, term_in, term_out = lax.cond(active, run_backward, skip_backward)
        grad_in = grad_in + term_in
        grad_out = grad_out + term_out
        cotangents = jnp.where(
            active, lax.dynamic_update_index_in_dim(cotangents, earlier, block_index, 0), cotangents
        )
        if timestep + 1 < turn_count:
            incoming = from_behind(earlier, "section", -1)
    shard_in, shard_out = (
        lax.psum_scatter(
            (grad_in * in_scale).astype(jnp.bfloat16), "fsdp", scatter_dimension=0, tiled=True
        ).astype(jnp.float32),
        lax.psum_scatter(
            (grad_out * out_scale).astype(jnp.bfloat16), "fsdp", scatter_dimension=1, tiled=True
        ).astype(jnp.float32),
    )
    fresh_in = fast_in[0] - fast_rate * shard_in
    fresh_out = fast_out[0] - fast_rate * shard_out
    synced_first = slow_in[0] + preview_mix * (fresh_in - slow_in[0])
    synced_second = slow_out[0] + preview_mix * (fresh_out - slow_out[0])
    section_out = produced.reshape(row_count, model_width)[None]
    input_grad = cotangents.reshape(row_count, model_width)[None]
    return (section_out, input_grad, synced_first[None], synced_second[None])


def solution(mesh):
    placed = (
        P("fsdp", None),
        P("fsdp", None),
        P("section", "fsdp", None),
        P("section", None, "fsdp"),
        P("section", "fsdp", None),
        P("section", None, "fsdp"),
    )
    return jax.shard_map(
        shards,
        mesh=mesh,
        in_specs=placed,
        out_specs=(
            P("section", "fsdp", None),
            P("section", "fsdp", None),
            P("section", "fsdp", None),
            P("section", None, "fsdp"),
        ),
        check_vma=False,
    )
```

profile of v0, /device:TPU:0, one launch (start us, length us, event | category | flops | bytes accessed | tf_op | source)
XLA Modules:
  0.0 1018.3 jit_solution(3030344230402729887)
XLA Ops:
  9.7 365.5 %all-gather.2.cloned.1.call-done = bf16[4096,2048]{1,0:T(8,128)(2,1)} async-done(((bf16[128,2048]{1,0:T(8,128)(2,1)}), bf16[4096,2048]{1,0:T(8,128)(2,1)}) %all-gather.2.cloned.1.call-update) | async-done | bytes 16777232 | tf_op jit(solution)/shard_map/all_gather | solution.py:16
  375.2 11.7 %slice_bitcast_fusion = (bf16[1024,4096]{0,1:T(8,128)(2,1)}, bf16[4096,1024]{1,0:T(8,128)(2,1)}) fusion(bf16[4096,2048]{1,0:T(8,128)(2,1)} %all-gather.2.cloned.1.call-done), kind=kLoop, calls=%fused_computation.146 | loop fusion | bytes 33554432 | tf_op jit(solution)/shard_map/transpose | solution.py:20
  386.9 10.2 conditional.8
  387.2 9.9 fusion
  398.5 2.2 collective-permute-done
  401.9 19.2 %collective-permute-start.1 = (bf16[128,4096]{1,0:T(8,128)(2,1)S(1)}, bf16[128,4096]{1,0:T(8,128)(2,1)S(1)}, u32[]{:S(2)}, u32[]{:S(2)}) collective-permute-start(bf16[128,4096]{1,0:T(8,128)(2,1)S(1)} %get-tuple-element.275), channel_id=1, source_target_pairs={{0,32},{32,64},{64,96},{1,33},{33,65},{65,97},{2,34},{34,66},{66,9... | collective-permute-start | bytes 3145736 | tf_op jit(solution)/shard_map/ppermute | solution.py:29
  421.1 2.2 collective-permute-done.1
  424.7 12.4 %collective-permute-start.2 = (bf16[128,4096]{1,0:T(8,128)(2,1)S(1)}, bf16[128,4096]{1,0:T(8,128)(2,1)}, u32[]{:S(2)}, u32[]{:S(2)}) collective-permute-start(bf16[128,4096]{1,0:T(8,128)(2,1)S(1)} %get-tuple-element.276), channel_id=1, source_target_pairs={{0,32},{32,64},{64,96},{1,33},{33,65},{65,97},{2,34},{34,66},{66,9... | collective-permute-start | bytes 3145736 | tf_op jit(solution)/shard_map/ppermute | solution.py:29
  439.7 16.1 %conditional.12 = (bf16[128,4096]{1,0:T(8,128)(2,1)S(1)}, f32[4096,1024]{1,0:T(8,128)}, f32[1024,4096]{0,1:T(8,128)}) conditional(s32[]{:T(128)} %convert_element_type.171, () %tuple.75, (pred[]{:T(512)}, bf16[128,4096]{1,0:T(8,128)(2,1)S(1)}, bf16[128,4096]{1,0:T(8,128)(2,1)S(1)}, bf16[128,4096]{1,0:T(8,128)(2,1)S(1)}, ...), branch_computations={%region_12.13_spmd, %region_13.16_spmd} | conditional | flops 5382078464 | bytes 128194168 | solution.py:142
  439.8 7.9 broadcast.228
  447.7 7.9 broadcast.229.clone
  457.2 29.5 %collective-permute-done.3 = bf16[128,4096]{1,0:T(8,128)(2,1)} collective-permute-done((bf16[128,4096]{1,0:T(8,128)(2,1)S(1)}, bf16[128,4096]{1,0:T(8,128)(2,1)}, u32[]{:S(2)}, u32[]{:S(2)}) %collective-permute-start.3) | collective-permute-done | bytes 1048608 | tf_op jit(solution)/shard_map/ppermute | solution.py:29
  486.7 16.4 %conditional.13 = (bf16[128,4096]{1,0:T(8,128)(2,1)S(1)}, f32[4096,1024]{1,0:T(8,128)}, f32[1024,4096]{0,1:T(8,128)}) conditional(s32[]{:T(128)} %convert_element_type.170, () %tuple.74, (pred[]{:T(512)}, bf16[128,4096]{1,0:T(8,128)(2,1)S(1)}, bf16[128,4096]{1,0:T(8,128)(2,1)}, bf16[128,4096]{1,0:T(8,128)(2,1)S(1)}, bf16[1024,4096]{0,1:T(8,128)(2,1)}, ...), branch_computations={%region_16.17_spmd, %region_17.20_spmd} | conditional | flops 5382078464 | bytes 128194168 | solution.py:142
  487.1 8.0 broadcast.234
  495.1 8.0 broadcast.235.clone
  504.5 17.3 %collective-permute-done.4 = bf16[128,4096]{1,0:T(8,128)(2,1)} collective-permute-done((bf16[128,4096]{1,0:T(8,128)(2,1)S(1)}, bf16[128,4096]{1,0:T(8,128)(2,1)}, u32[]{:S(2)}, u32[]{:S(2)}) %collective-permute-start.4) | collective-permute-done | bytes 1048608 | tf_op jit(solution)/shard_map/ppermute | solution.py:29
  521.7 17.0 %conditional.14 = (bf16[128,4096]{1,0:T(8,128)(2,1)}, f32[4096,1024]{1,0:T(8,128)}, f32[1024,4096]{0,1:T(8,128)}) conditional(s32[]{:T(128)} %convert_element_type.169, () %tuple.73, (pred[]{:T(512)}, bf16[128,4096]{1,0:T(8,128)(2,1)S(1)}, bf16[128,4096]{1,0:T(8,128)(2,1)}, bf16[128,4096]{1,0:T(8,128)(2,1)S(1)}, bf16[1024,4096]{0,1:T(8,128)(2,1)}, ...), branch_computations={%region_20.21_spmd, %region_21.24_spmd} | conditional | flops 5382078464 | bytes 128194168 | solution.py:142
  521.9 7.9 broadcast.240
  529.8 7.9 broadcast.241.clone
  540.0 37.3 %collective-permute-done.5 = bf16[128,4096]{1,0:T(8,128)(2,1)} collective-permute-done((bf16[128,4096]{1,0:T(8,128)(2,1)}, bf16[128,4096]{1,0:T(8,128)(2,1)}, u32[]{:S(2)}, u32[]{:S(2)}) %collective-permute-start.5) | collective-permute-done | bytes 1048608 | tf_op jit(solution)/shard_map/ppermute | solution.py:29
  577.4 29.4 %conditional.15 = (bf16[128,4096]{1,0:T(8,128)(2,1)}, f32[4096,1024]{1,0:T(8,128)}, f32[1024,4096]{0,1:T(8,128)}) conditional(s32[]{:T(128)} %convert_element_type.168, () %tuple.72, (pred[]{:T(512)}, bf16[128,4096]{1,0:T(8,128)(2,1)S(1)}, bf16[128,4096]{1,0:T(8,128)(2,1)}, bf16[128,4096]{1,0:T(8,128)(2,1)S(1)}, bf16[1024,4096]{0,1:T(8,128)(2,1)}, ...), branch_computations={%region_24.25_spmd, %region_25.28_spmd} | conditional | flops 5382078464 | bytes 128194168 | solution.py:142
  577.9 4.8 fusion.115
  585.6 8.2 fusion.113
  593.8 3.0 fusion.105
  596.8 1.6 fusion.109
  598.4 8.1 fusion.117
  606.8 26.0 %multiply_convert_fusion.12 = bf16[1024,4096]{0,1:T(8,128)(2,1)} fusion(f32[1024,4096]{0,1:T(8,128)} %get-tuple-element.235, f32[1024,4096]{0,1:T(8,128)} %get-tuple-element.234, f32[1024,4096]{0,1:T(8,128)} %get-tuple-element.232, f32[1024,4096]{0,1:T(8,128)} %get-tuple-element.233), kind=kLoop, calls=%fused_computation.144 | loop fusion | flops 20971520 | bytes 75497472 | tf_op jit(solution)/shard_map/convert_element_type | solution.py:155
  632.8 26.3 %multiply_convert_fusion.13 = bf16[4096,1024]{1,0:T(8,128)(2,1)} fusion(f32[4096,1024]{1,0:T(8,128)} %get-tuple-element.151, f32[4096,1024]{1,0:T(8,128)} %get-tuple-element.150, f32[4096,1024]{1,0:T(8,128)} %get-tuple-element.148, f32[4096,1024]{1,0:T(8,128)} %get-tuple-element.149), kind=kLoop, calls=%fused_computation.145 | loop fusion | flops 20971520 | bytes 75497472 | tf_op jit(solution)/shard_map/convert_element_type | solution.py:152
  662.8 3.3 select_bitcast_fusion
  666.1 152.7 %reduce-scatter.5.cloned.1.call-done = bf16[1024,128]{0,1:T(8,128)(2,1)} async-done(((bf16[1024,4096]{0,1:T(8,128)(2,1)}), bf16[1024,128]{0,1:T(8,128)(2,1)}) %reduce-scatter.5.cloned.1.call-update) | async-done | bytes 262160 | tf_op jit(solution)/shard_map/reduce_scatter | solution.py:154
  820.9 188.6 %reduce-scatter.3.cloned.1.call-done = bf16[128,1024]{1,0:T(8,128)(2,1)} async-done(((bf16[4096,1024]{1,0:T(8,128)(2,1)}), bf16[128,1024]{1,0:T(8,128)(2,1)}) %reduce-scatter.3.cloned.1.call-update) | async-done | bytes 262160 | tf_op jit(solution)/shard_map/reduce_scatter | solution.py:151
  1009.5 1.9 fusion.123
  (79 shorter events, 23.7 us)
Async XLA Ops:
  7.2 1.5 copy-start.10
  7.2 2.5 copy-start.1
  7.2 368.1 %all-gather.2.cloned.1.call-start = ((), (), s32[]{:S(2)}) async-start(), calls=%async_computation.2 | async-start | bytes 17301504 | tf_op jit(solution)/shard_map/all_gather | solution.py:16
  8.6 1.1 copy-start.2
  9.6 809.3 %reduce-scatter.5.cloned.1.call-start = ((), (), s32[]{:S(2)}) async-start(), calls=%async_computation.4 | async-start | bytes 8650752 | tf_op jit(solution)/shard_map/reduce_scatter | solution.py:154
  397.1 4.7 copy-start.6
  397.1 3.6 collective-permute-start
  401.9 22.5 %copy-start.7 = (bf16[128,4096]{1,0:T(8,128)(2,1)}, bf16[128,4096]{1,0:T(8,128)(2,1)S(1)}, u32[]{:S(2)}) copy-start(bf16[128,4096]{1,0:T(8,128)(2,1)S(1)} %get-tuple-element.275) | copy-start | bytes 3145732
  401.9 21.4 %collective-permute-start.1 = (bf16[128,4096]{1,0:T(8,128)(2,1)S(1)}, bf16[128,4096]{1,0:T(8,128)(2,1)S(1)}, u32[]{:S(2)}, u32[]{:S(2)}) collective-permute-start(bf16[128,4096]{1,0:T(8,128)(2,1)S(1)} %get-tuple-element.275), channel_id=1, source_target_pairs={{0,32},{32,64},{64,96},{1,33},{33,65},{65,97},{2,34},{34,66},{66,9... | collective-permute-start | bytes 3145736 | tf_op jit(solution)/shard_map/ppermute | solution.py:29
  424.7 12.4 %copy-start.8 = (bf16[128,4096]{1,0:T(8,128)(2,1)}, bf16[128,4096]{1,0:T(8,128)(2,1)S(1)}, u32[]{:S(2)}) copy-start(bf16[128,4096]{1,0:T(8,128)(2,1)S(1)} %get-tuple-element.276) | copy-start | bytes 3145732
  424.7 13.8 %collective-permute-start.2 = (bf16[128,4096]{1,0:T(8,128)(2,1)S(1)}, bf16[128,4096]{1,0:T(8,128)(2,1)}, u32[]{:S(2)}, u32[]{:S(2)}) collective-permute-start(bf16[128,4096]{1,0:T(8,128)(2,1)S(1)} %get-tuple-element.276), channel_id=1, source_target_pairs={{0,32},{32,64},{64,96},{1,33},{33,65},{65,97},{2,34},{34,66},{66,9... | collective-permute-start | bytes 3145736 | tf_op jit(solution)/shard_map/ppermute | solution.py:29
  437.0 2.7 copy-start
  455.9 30.8 %copy-start.4 = (bf16[128,4096]{1,0:T(8,128)(2,1)}, bf16[128,4096]{1,0:T(8,128)(2,1)S(1)}, u32[]{:S(2)}) copy-start(bf16[128,4096]{1,0:T(8,128)(2,1)S(1)} %get-tuple-element.144) | copy-start | bytes 3145732
  455.9 30.8 %collective-permute-start.3 = (bf16[128,4096]{1,0:T(8,128)(2,1)S(1)}, bf16[128,4096]{1,0:T(8,128)(2,1)}, u32[]{:S(2)}, u32[]{:S(2)}) collective-permute-start(bf16[128,4096]{1,0:T(8,128)(2,1)S(1)} %get-tuple-element.144), channel_id=1, source_target_pairs={{32,0},{64,32},{96,64},{33,1},{65,33},{97,65},{34,2},{66,34},{98,6... | collective-permute-start | bytes 3145736 | tf_op jit(solution)/shard_map/ppermute | solution.py:29
  503.2 18.6 %collective-permute-start.4 = (bf16[128,4096]{1,0:T(8,128)(2,1)S(1)}, bf16[128,4096]{1,0:T(8,128)(2,1)}, u32[]{:S(2)}, u32[]{:S(2)}) collective-permute-start(bf16[128,4096]{1,0:T(8,128)(2,1)S(1)} %get-tuple-element.145), channel_id=1, source_target_pairs={{32,0},{64,32},{96,64},{33,1},{65,33},{97,65},{34,2},{66,34},{98,6... | collective-permute-start | bytes 3145736 | tf_op jit(solution)/shard_map/ppermute | solution.py:29
  538.7 38.6 %collective-permute-start.5 = (bf16[128,4096]{1,0:T(8,128)(2,1)}, bf16[128,4096]{1,0:T(8,128)(2,1)}, u32[]{:S(2)}, u32[]{:S(2)}) collective-permute-start(bf16[128,4096]{1,0:T(8,128)(2,1)} %get-tuple-element.146), channel_id=1, source_target_pairs={{32,0},{64,32},{96,64},{33,1},{65,33},{97,65},{34,2},{66,34},{98,6... | collective-permute-start | bytes 3145736 | tf_op jit(solution)/shard_map/ppermute | solution.py:29
  577.9 6.2 slice-start.14
  577.9 6.2 slice-start.15
  584.1 9.7 slice-start.6
  585.6 8.2 slice-start.7
  632.8 376.7 %reduce-scatter.3.cloned.1.call-start = ((), (), s32[]{:S(2)}) async-start(), calls=%async_computation.3 | async-start | bytes 8650752 | tf_op jit(solution)/shard_map/reduce_scatter | solution.py:151
  659.1 1.0 copy-start.14
  661.2 1.6 copy-start.5
  661.3 1.0 copy-start.9
  662.8 156.1 %copy-start.3 = (f32[1,1024,128]{1,2,0:T(8,128)S(1)}, f32[1,1024,128]{1,2,0:T(8,128)}, u32[]{:S(2)}) copy-start(f32[1,1024,128]{1,2,0:T(8,128)} %copy-done.2) | copy-start | bytes 1572868
  662.8 156.1 %copy-start.12 = (f32[1,1024,128]{1,2,0:T(8,128)S(1)}, f32[1,1024,128]{1,2,0:T(8,128)}, u32[]{:S(2)}) copy-start(f32[1,1024,128]{1,2,0:T(8,128)} %copy.33) | copy-start | bytes 1572868
  666.1 343.4 %copy-start.11 = (f32[1,128,1024]{2,1,0:T(8,128)S(1)}, f32[1,128,1024]{2,1,0:T(8,128)}, u32[]{:S(2)}) copy-start(f32[1,128,1024]{2,1,0:T(8,128)} %param.24) | copy-start | bytes 1572868
  666.1 343.4 %copy-start.13 = (f32[1,128,1024]{2,1,0:T(8,128)S(1)}, f32[1,128,1024]{2,1,0:T(8,128)}, u32[]{:S(2)}) copy-start(f32[1,128,1024]{2,1,0:T(8,128)} %param.26) | copy-start | bytes 1572868
Sparse Core Ops, SparseCore 0:
  10.2 364.9 all-gather.1
  632.9 185.8 reduce-scatter.4
  821.3 188.1 reduce-scatter.2
where the time goes:
time: 1030 us; the launch traced here: 1020 us
  waiting for transfers between devices  797 us (77%)
  local copies, waits for them, and re-layouts  66.7 us (6%)
  other arithmetic  66.4 us (6%)
  starting transfers between devices  36.9 us (4%)
  matrix products  35.5 us (3%)
  between operations  14.5 us (1%)
    all_gather x1, waiting for transfers between devices, gather_turned(): result = lax.all_gather(both, axis, axis=0, tiled=True)  366 us
    reduce_scatter x1, waiting for transfers between devices, shards(): lax.psum_scatter((grad_in * in_scale).astype(jnp.bfloat16), 'fsdp', scatt...  189 us
    reduce_scatter x1, waiting for transfers between devices, shards(): lax.psum_scatter((grad_out * out_scale).astype(jnp.bfloat16), 'fsdp', sca...  153 us
    ppermute x6, waiting for transfers between devices, from_behind(): lax.ppermute(value, axis, [(source, source + steps) for source in range(l...  89.9 us
    another operation x13, local copies, waits for them, and re-layouts  49.1 us
    ppermute x6, starting transfers between devices, from_behind(): lax.ppermute(value, axis, [(source, source + steps) for source in range(l...  36.8 us
    convert_element_type x1, other arithmetic, shards(): (grad_in * in_scale).astype(jnp.bfloat16)  26.3 us
    convert_element_type x1, other arithmetic, shards(): (grad_out * out_scale).astype(jnp.bfloat16)  26 us
  transfers between devices with their start and end apart: 9, of which 9 were waited for; matrix products, arithmetic and copies ran while one was open for 3% of the time, Pallas kernels for 0%

commit v1 on v0

--- a/solution.py
+++ b/solution.py
@@ -13,7 +13,9 @@
     turned = [jnp.moveaxis(a, dim, 0) for a, dim in zip(arrays, dims)]
     widths = [t[0].size for t in turned]
     both = jnp.concatenate([t.reshape(-1, w) for t, w in zip(turned, widths)], axis=1)
-    result = lax.all_gather(both, axis, axis=0, tiled=True)
+    result = jnp.concatenate(
+        lax.all_to_all(jnp.stack([both] * lax.axis_size(axis)), axis, 0, 0), axis=0
+    )
     pieces = jnp.split(result, [sum(widths[:k]) for k in range(1, len(widths))], axis=1)
     return tuple(
         (

time: 1030 us -> 956 us (0.928)
  waiting for transfers between devices: 797 us -> 715 us
    all_gather x1 -> x0, waiting for transfers between devices: 366 us -> none  [gather_turned(): result = lax.all_gather(both, axis, axis=0, tiled=True)]
    all_to_all x0 -> x1, waiting for transfers between devices: none -> 269 us  [gather_turned(): lax.all_to_all(jnp.stack([both] * lax.axis_size(axis)), axis, 0, 0)]
    reduce_scatter x1, waiting for transfers between devices: 153 us -> 167 us  [shards(): lax.psum_scatter((grad_out * out_scale).astype(jnp.bfloat16), 'fsdp', sca...]
    another operation x13 -> x14, local copies, waits for them, and re-layouts: 49.1 us -> 55.3 us
where the time goes in v1:
time: 956 us; the launch traced here: 949 us
  waiting for transfers between devices  715 us (75%)
  local copies, waits for them, and re-layouts  72.8 us (8%)
  other arithmetic  65.3 us (7%)
  starting transfers between devices  44 us (5%)
  matrix products  35.5 us (4%)
  between operations  14.8 us (2%)
    all_to_all x1, waiting for transfers between devices, gather_turned(): lax.all_to_all(jnp.stack([both] * lax.axis_size(axis)), axis, 0, 0)  269 us
    reduce_scatter x1, waiting for transfers between devices, shards(): lax.psum_scatter((grad_in * in_scale).astype(jnp.bfloat16), 'fsdp', scatt...  188 us
    reduce_scatter x1, waiting for transfers between devices, shards(): lax.psum_scatter((grad_out * out_scale).astype(jnp.bfloat16), 'fsdp', sca...  167 us
    ppermute x6, waiting for transfers between devices, from_behind(): lax.ppermute(value, axis, [(source, source + steps) for source in range(l...  89.9 us
    another operation x13, local copies, waits for them, and re-layouts  49.2 us
    ppermute x6, starting transfers between devices, from_behind(): lax.ppermute(value, axis, [(source, source + steps) for source in range(l...  34.4 us
    convert_element_type x1, other arithmetic, shards(): (grad_in * in_scale).astype(jnp.bfloat16)  26.1 us
    convert_element_type x1, other arithmetic, shards(): (grad_out * out_scale).astype(jnp.bfloat16)  26 us
  transfers between devices with their start and end apart: 9, of which 9 were waited for; matrix products, arithmetic and copies ran while one was open for 3% of the time, Pallas kernels for 0%

profile of v1, /device:TPU:0, one launch (start us, length us, event | category | flops | bytes accessed | tf_op | source)
XLA Modules:
  0.0 948.7 jit_solution(2325944529418079807)
XLA Ops:
  8.6 6.1 stack.2
  14.8 9.5 %all-to-all-start = ((bf16[32,128,2048]{2,1,0:T(8,128)(2,1)}), bf16[32,128,2048]{2,1,0:T(8,128)(2,1)}, u32[]{:S(2)}, u32[]{:S(2)}) async-start(bf16[32,128,2048]{2,1,0:T(8,128)(2,1)} %stack.2), calls=%async_computation | async-start | bytes 33554432 | tf_op jit(solution)/shard_map/all_to_all | solution.py:17
  24.5 269.1 %all-to-all-done = bf16[32,128,2048]{2,1,0:T(8,128)(2,1)} async-done(((bf16[32,128,2048]{2,1,0:T(8,128)(2,1)}), bf16[32,128,2048]{2,1,0:T(8,128)(2,1)}, u32[]{:S(2)}, u32[]{:S(2)}) %all-to-all-start) | async-done | bytes 16777248 | tf_op jit(solution)/shard_map/all_to_all | solution.py:17
  293.6 11.7 %slice_bitcast_fusion = (bf16[1024,4096]{0,1:T(8,128)(2,1)}, bf16[4096,1024]{1,0:T(8,128)(2,1)}) fusion(bf16[4096,2048]{1,0:T(8,128)(2,1)} %bitcast.3), kind=kLoop, calls=%fused_computation.146 | loop fusion | bytes 33554432 | tf_op jit(solution)/shard_map/transpose | solution.py:22
  305.3 10.2 %conditional.8 = (bf16[128,4096]{1,0:T(8,128)(2,1)S(1)}) conditional(s32[]{:T(128)} %convert_element_type.165, () %tuple.67, (bf16[128,4096]{1,0:T(8,128)(2,1)S(1)}, bf16[4096,1024]{1,0:T(8,128)(2,1)}, bf16[1024,4096]{0,1:T(8,128)(2,1)}) %tuple.68), branch_computations={%region_0.1_spmd, %region_1.3_spmd} | conditional | flops 2152857600 | bytes 19925000 | solution.py:109
  305.6 9.9 %fusion = bf16[128,4096]{1,0:T(8,128)(2,1)S(1)} fusion(bf16[1024,4096]{0,1:T(8,128)(2,1)} %get-tuple-element.194, bf16[128,4096]{1,0:T(8,128)(2,1)S(1)} %get-tuple-element.92, bf16[4096,1024]{1,0:T(8,128)(2,1)} %get-tuple-element.93, f32[128]{0:T(128)S(1)} %add_rsqrt_fusion), kind=kOutput, calls=%fused_computation.1 | convolution fusion | flops 2151284736 | bytes 18874880 | tf_op jit(solution)/shard_map/cond/branch_1_fun/dot_general | solution.py:57
  316.8 2.2 collective-permute-done
  320.2 16.8 %collective-permute-start.1 = (bf16[128,4096]{1,0:T(8,128)(2,1)S(1)}, bf16[128,4096]{1,0:T(8,128)(2,1)S(1)}, u32[]{:S(2)}, u32[]{:S(2)}) collective-permute-start(bf16[128,4096]{1,0:T(8,128)(2,1)S(1)} %get-tuple-element.275), channel_id=1, source_target_pairs={{0,32},{32,64},{64,96},{1,33},{33,65},{65,97},{2,34},{34,66},{66,9... | collective-permute-start | bytes 3145736 | tf_op jit(solution)/shard_map/ppermute | solution.py:31
  337.0 2.2 collective-permute-done.1
  340.6 12.4 %collective-permute-start.2 = (bf16[128,4096]{1,0:T(8,128)(2,1)S(1)}, bf16[128,4096]{1,0:T(8,128)(2,1)}, u32[]{:S(2)}, u32[]{:S(2)}) collective-permute-start(bf16[128,4096]{1,0:T(8,128)(2,1)S(1)} %get-tuple-element.276), channel_id=1, source_target_pairs={{0,32},{32,64},{64,96},{1,33},{33,65},{65,97},{2,34},{34,66},{66,9... | collective-permute-start | bytes 3145736 | tf_op jit(solution)/shard_map/ppermute | solution.py:31
  355.7 16.1 %conditional.12 = (bf16[128,4096]{1,0:T(8,128)(2,1)S(1)}, f32[4096,1024]{1,0:T(8,128)}, f32[1024,4096]{0,1:T(8,128)}) conditional(s32[]{:T(128)} %convert_element_type.171, () %tuple.75, (pred[]{:T(512)}, bf16[128,4096]{1,0:T(8,128)(2,1)S(1)}, bf16[128,4096]{1,0:T(8,128)(2,1)S(1)}, bf16[128,4096]{1,0:T(8,128)(2,1)S(1)}, ...), branch_computations={%region_12.13_spmd, %region_13.16_spmd} | conditional | flops 5382078464 | bytes 128194168 | solution.py:144
  355.7 7.9 broadcast.230
  363.6 7.9 broadcast.231.clone
  373.1 29.5 %collective-permute-done.3 = bf16[128,4096]{1,0:T(8,128)(2,1)} collective-permute-done((bf16[128,4096]{1,0:T(8,128)(2,1)S(1)}, bf16[128,4096]{1,0:T(8,128)(2,1)}, u32[]{:S(2)}, u32[]{:S(2)}) %collective-permute-start.3) | collective-permute-done | bytes 1048608 | tf_op jit(solution)/shard_map/ppermute | solution.py:31
  402.6 16.5 %conditional.13 = (bf16[128,4096]{1,0:T(8,128)(2,1)S(1)}, f32[4096,1024]{1,0:T(8,128)}, f32[1024,4096]{0,1:T(8,128)}) conditional(s32[]{:T(128)} %convert_element_type.170, () %tuple.74, (pred[]{:T(512)}, bf16[128,4096]{1,0:T(8,128)(2,1)S(1)}, bf16[128,4096]{1,0:T(8,128)(2,1)}, bf16[128,4096]{1,0:T(8,128)(2,1)S(1)}, bf16[1024,4096]{0,1:T(8,128)(2,1)}, ...), branch_computations={%region_16.17_spmd, %region_17.20_spmd} | conditional | flops 5382078464 | bytes 128194168 | solution.py:144
  403.0 8.0 broadcast.236
  411.0 8.0 broadcast.237.clone
  420.4 17.3 %collective-permute-done.4 = bf16[128,4096]{1,0:T(8,128)(2,1)} collective-permute-done((bf16[128,4096]{1,0:T(8,128)(2,1)S(1)}, bf16[128,4096]{1,0:T(8,128)(2,1)}, u32[]{:S(2)}, u32[]{:S(2)}) %collective-permute-start.4) | collective-permute-done | bytes 1048608 | tf_op jit(solution)/shard_map/ppermute | solution.py:31
  437.7 17.0 %conditional.14 = (bf16[128,4096]{1,0:T(8,128)(2,1)}, f32[4096,1024]{1,0:T(8,128)}, f32[1024,4096]{0,1:T(8,128)}) conditional(s32[]{:T(128)} %convert_element_type.169, () %tuple.73, (pred[]{:T(512)}, bf16[128,4096]{1,0:T(8,128)(2,1)S(1)}, bf16[128,4096]{1,0:T(8,128)(2,1)}, bf16[128,4096]{1,0:T(8,128)(2,1)S(1)}, bf16[1024,4096]{0,1:T(8,128)(2,1)}, ...), branch_computations={%region_20.21_spmd, %region_21.24_spmd} | conditional | flops 5382078464 | bytes 128194168 | solution.py:144
  437.9 7.9 broadcast.242
  445.7 7.9 broadcast.243.clone
  456.0 37.3 %collective-permute-done.5 = bf16[128,4096]{1,0:T(8,128)(2,1)} collective-permute-done((bf16[128,4096]{1,0:T(8,128)(2,1)}, bf16[128,4096]{1,0:T(8,128)(2,1)}, u32[]{:S(2)}, u32[]{:S(2)}) %collective-permute-start.5) | collective-permute-done | bytes 1048608 | tf_op jit(solution)/shard_map/ppermute | solution.py:31
  493.3 29.4 %conditional.15 = (bf16[128,4096]{1,0:T(8,128)(2,1)}, f32[4096,1024]{1,0:T(8,128)}, f32[1024,4096]{0,1:T(8,128)}) conditional(s32[]{:T(128)} %convert_element_type.168, () %tuple.72, (pred[]{:T(512)}, bf16[128,4096]{1,0:T(8,128)(2,1)S(1)}, bf16[128,4096]{1,0:T(8,128)(2,1)}, bf16[128,4096]{1,0:T(8,128)(2,1)S(1)}, bf16[1024,4096]{0,1:T(8,128)(2,1)}, ...), branch_computations={%region_24.25_spmd, %region_25.28_spmd} | conditional | flops 5382078464 | bytes 128194168 | solution.py:144
  493.8 4.8 fusion.115
  501.6 8.2 fusion.113
  509.8 3.0 fusion.105
  514.3 8.1 fusion.117
  522.7 26.0 %multiply_convert_fusion.12 = bf16[1024,4096]{0,1:T(8,128)(2,1)} fusion(f32[1024,4096]{0,1:T(8,128)} %get-tuple-element.235, f32[1024,4096]{0,1:T(8,128)} %get-tuple-element.234, f32[1024,4096]{0,1:T(8,128)} %get-tuple-element.232, f32[1024,4096]{0,1:T(8,128)} %get-tuple-element.233), kind=kLoop, calls=%fused_computation.144 | loop fusion | flops 20971520 | bytes 75497472 | tf_op jit(solution)/shard_map/convert_element_type | solution.py:157
  548.8 26.1 %multiply_convert_fusion.13 = bf16[4096,1024]{1,0:T(8,128)(2,1)} fusion(f32[4096,1024]{1,0:T(8,128)} %get-tuple-element.151, f32[4096,1024]{1,0:T(8,128)} %get-tuple-element.150, f32[4096,1024]{1,0:T(8,128)} %get-tuple-element.148, f32[4096,1024]{1,0:T(8,128)} %get-tuple-element.149), kind=kLoop, calls=%fused_computation.145 | loop fusion | flops 20971520 | bytes 75497472 | tf_op jit(solution)/shard_map/convert_element_type | solution.py:154
  578.5 3.3 select_bitcast_fusion
  581.8 167.4 %reduce-scatter.5.cloned.1.call-done = bf16[1024,128]{0,1:T(8,128)(2,1)} async-done(((bf16[1024,4096]{0,1:T(8,128)(2,1)}), bf16[1024,128]{0,1:T(8,128)(2,1)}) %reduce-scatter.5.cloned.1.call-update) | async-done | bytes 262160 | tf_op jit(solution)/shard_map/reduce_scatter | solution.py:156
  751.3 188.3 %reduce-scatter.3.cloned.1.call-done = bf16[128,1024]{1,0:T(8,128)(2,1)} async-done(((bf16[4096,1024]{1,0:T(8,128)(2,1)}), bf16[128,1024]{1,0:T(8,128)(2,1)}) %reduce-scatter.3.cloned.1.call-update) | async-done | bytes 262160 | tf_op jit(solution)/shard_map/reduce_scatter | solution.py:153
  (79 shorter events, 26.2 us)
Async XLA Ops:
  7.2 1.4 copy-start.10
  8.5 6.3 copy-start.2
  14.8 9.6 %copy-start.1 = (bf16[128,4096]{1,0:T(8,128)(2,1)S(1)}, bf16[128,4096]{1,0:T(8,128)(2,1)}, u32[]{:S(2)}) copy-start(bf16[128,4096]{1,0:T(8,128)(2,1)} %param.22) | copy-start | bytes 3145732
  14.8 278.8 %all-to-all-start = ((bf16[32,128,2048]{2,1,0:T(8,128)(2,1)}), bf16[32,128,2048]{2,1,0:T(8,128)(2,1)}, u32[]{:S(2)}, u32[]{:S(2)}) async-start(bf16[32,128,2048]{2,1,0:T(8,128)(2,1)} %stack.2), calls=%async_computation | async-start | bytes 33554432 | tf_op jit(solution)/shard_map/all_to_all | solution.py:17
  24.3 724.9 %reduce-scatter.5.cloned.1.call-start = ((), (), s32[]{:S(2)}) async-start(), calls=%async_computation.4 | async-start | bytes 8650752 | tf_op jit(solution)/shard_map/reduce_scatter | solution.py:156
  315.5 4.7 copy-start.6
  315.5 3.6 collective-permute-start
  320.2 20.1 %copy-start.7 = (bf16[128,4096]{1,0:T(8,128)(2,1)}, bf16[128,4096]{1,0:T(8,128)(2,1)S(1)}, u32[]{:S(2)}) copy-start(bf16[128,4096]{1,0:T(8,128)(2,1)S(1)} %get-tuple-element.275) | copy-start | bytes 3145732
  320.2 19.0 %collective-permute-start.1 = (bf16[128,4096]{1,0:T(8,128)(2,1)S(1)}, bf16[128,4096]{1,0:T(8,128)(2,1)S(1)}, u32[]{:S(2)}, u32[]{:S(2)}) collective-permute-start(bf16[128,4096]{1,0:T(8,128)(2,1)S(1)} %get-tuple-element.275), channel_id=1, source_target_pairs={{0,32},{32,64},{64,96},{1,33},{33,65},{65,97},{2,34},{34,66},{66,9... | collective-permute-start | bytes 3145736 | tf_op jit(solution)/shard_map/ppermute | solution.py:31
  340.6 12.4 %copy-start.8 = (bf16[128,4096]{1,0:T(8,128)(2,1)}, bf16[128,4096]{1,0:T(8,128)(2,1)S(1)}, u32[]{:S(2)}) copy-start(bf16[128,4096]{1,0:T(8,128)(2,1)S(1)} %get-tuple-element.276) | copy-start | bytes 3145732
  340.6 13.8 %collective-permute-start.2 = (bf16[128,4096]{1,0:T(8,128)(2,1)S(1)}, bf16[128,4096]{1,0:T(8,128)(2,1)}, u32[]{:S(2)}, u32[]{:S(2)}) collective-permute-start(bf16[128,4096]{1,0:T(8,128)(2,1)S(1)} %get-tuple-element.276), channel_id=1, source_target_pairs={{0,32},{32,64},{64,96},{1,33},{33,65},{65,97},{2,34},{34,66},{66,9... | collective-permute-start | bytes 3145736 | tf_op jit(solution)/shard_map/ppermute | solution.py:31
  353.0 2.7 copy-start
  371.8 30.8 %copy-start.4 = (bf16[128,4096]{1,0:T(8,128)(2,1)}, bf16[128,4096]{1,0:T(8,128)(2,1)S(1)}, u32[]{:S(2)}) copy-start(bf16[128,4096]{1,0:T(8,128)(2,1)S(1)} %get-tuple-element.144) | copy-start | bytes 3145732
  371.8 30.8 %collective-permute-start.3 = (bf16[128,4096]{1,0:T(8,128)(2,1)S(1)}, bf16[128,4096]{1,0:T(8,128)(2,1)}, u32[]{:S(2)}, u32[]{:S(2)}) collective-permute-start(bf16[128,4096]{1,0:T(8,128)(2,1)S(1)} %get-tuple-element.144), channel_id=1, source_target_pairs={{32,0},{64,32},{96,64},{33,1},{65,33},{97,65},{34,2},{66,34},{98,6... | collective-permute-start | bytes 3145736 | tf_op jit(solution)/shard_map/ppermute | solution.py:31
  419.1 18.6 %collective-permute-start.4 = (bf16[128,4096]{1,0:T(8,128)(2,1)S(1)}, bf16[128,4096]{1,0:T(8,128)(2,1)}, u32[]{:S(2)}, u32[]{:S(2)}) collective-permute-start(bf16[128,4096]{1,0:T(8,128)(2,1)S(1)} %get-tuple-element.145), channel_id=1, source_target_pairs={{32,0},{64,32},{96,64},{33,1},{65,33},{97,65},{34,2},{66,34},{98,6... | collective-permute-start | bytes 3145736 | tf_op jit(solution)/shard_map/ppermute | solution.py:31
  454.7 38.6 %collective-permute-start.5 = (bf16[128,4096]{1,0:T(8,128)(2,1)}, bf16[128,4096]{1,0:T(8,128)(2,1)}, u32[]{:S(2)}, u32[]{:S(2)}) collective-permute-start(bf16[128,4096]{1,0:T(8,128)(2,1)} %get-tuple-element.146), channel_id=1, source_target_pairs={{32,0},{64,32},{96,64},{33,1},{65,33},{97,65},{34,2},{66,34},{98,6... | collective-permute-start | bytes 3145736 | tf_op jit(solution)/shard_map/ppermute | solution.py:31
  493.8 6.2 slice-start.14
  493.8 6.2 slice-start.15
  500.0 9.7 %slice-start.6 = ((s8[8388608]{0:T(1024)(128)(4,1)}), s8[4194304]{0:T(1024)(128)(4,1)S(1)}, s32[]{:S(2)}) async-start(s8[8388608]{0:T(1024)(128)(4,1)} %bitcast.89), calls=%async_computation.11 | async-start | bytes 8388608 | tf_op jit(solution)/shard_map/cond
  501.5 8.2 slice-start.7
  548.7 390.9 %reduce-scatter.3.cloned.1.call-start = ((), (), s32[]{:S(2)}) async-start(), calls=%async_computation.3 | async-start | bytes 8650752 | tf_op jit(solution)/shard_map/reduce_scatter | solution.py:153
  574.9 1.0 copy-start.14
  576.9 1.6 copy-start.5
  577.0 1.0 copy-start.9
  578.5 170.7 %copy-start.3 = (f32[1,1024,128]{1,2,0:T(8,128)S(1)}, f32[1,1024,128]{1,2,0:T(8,128)}, u32[]{:S(2)}) copy-start(f32[1,1024,128]{1,2,0:T(8,128)} %copy-done.2) | copy-start | bytes 1572868
  578.5 170.7 %copy-start.12 = (f32[1,1024,128]{1,2,0:T(8,128)S(1)}, f32[1,1024,128]{1,2,0:T(8,128)}, u32[]{:S(2)}) copy-start(f32[1,1024,128]{1,2,0:T(8,128)} %copy.34) | copy-start | bytes 1572868
  581.8 357.8 %copy-start.11 = (f32[1,128,1024]{2,1,0:T(8,128)S(1)}, f32[1,128,1024]{2,1,0:T(8,128)}, u32[]{:S(2)}) copy-start(f32[1,128,1024]{2,1,0:T(8,128)} %param.24) | copy-start | bytes 1572868
  581.8 357.8 %copy-start.13 = (f32[1,128,1024]{2,1,0:T(8,128)S(1)}, f32[1,128,1024]{2,1,0:T(8,128)}, u32[]{:S(2)}) copy-start(f32[1,128,1024]{2,1,0:T(8,128)} %param.26) | copy-start | bytes 1572868
Sparse Core Ops, SparseCore 0:
  548.8 200.3 reduce-scatter.4
  751.6 187.9 reduce-scatter.2
